TPU v7x, 128 devices: a whole 4x4x4 slice. The times are simulated.
128 devices in a mesh: row: 4 (over z), col: 2 (over y_lo), ex: 16 (over x, y_hi, core).
Axes of the slice: x: 4, y: 4 (y_hi: 2, y_lo: 2; y = y_hi * 2 + y_lo), z: 4, core: 2. Of those that a mesh axis runs over, the one named last changes fastest.
Arguments:
- train_in: bfloat16 [8192, 8192], P('ex', 'row'), may hold values from -6 to 6
- train_out: bfloat16 [8192, 8192], P('ex', 'col'), may hold values from -0.0047912598 to 0.0047912598
- query_in: bfloat16 [512, 8192], P('ex', 'row'), may hold values from -6 to 6
- query_out: bfloat16 [512, 8192], P('ex', 'col'), may hold values from -0.023925781 to 0.023925781
- query_ids: int32 [512], P('ex'), may hold values from 0 to 1
- in_basis: bfloat16 [8, 1024, 1024], P('row'), may hold values from -1 to 1, as said below
- out_basis: bfloat16 [8, 1024, 1024], P('col'), may hold values from -1 to 1, as said below
- level_table: float32 [64, 64], replicated, may hold values from 0.5 to 8
- in_level: int32 [8192], P('row'), may hold values from 0 to 63
- out_level: int32 [8192], P('col'), may hold values from 0 to 63
- lengths: int32 [4], replicated, may hold values from 1 to 4096, 8192 in all
Outputs:
- token_scores: float32 [2, 8192], P(None, 'ex')
- example_scores: float32 [2, 4], replicated
Inputs may be any that keep to these rules, and one draw needn't show every extreme that they name: `in_basis`: each block is an orthogonal matrix rounded to bfloat16. `out_basis`: each block is an orthogonal matrix rounded to bfloat16. `lengths`: the counts sum to 8192.
All inputs are finite; a program needn't handle non-finite values.
Results may differ from a plain program's by a relative error of at most 0.018.
Values may be sent and summed in bfloat16 or wider, within the bound.
No kernel may reach another device: no remote copies, remote signals or barrier semaphores. Data moves between devices by JAX's collectives and lax.ppermute only.
A program may use at most 192 MiB of HBM per device.

v0:
```python
import math
import jax
import jax.numpy as jnp
from jax import lax
from jax.sharding import PartitionSpec as P

QUERIES = 2
DAMPING = 0.1


def sent_together(arrays, axis, dim, along):
    widths = [math.prod(a.shape[along:]) for a in arrays]
    both = jnp.concatenate(
        [a.reshape(*a.shape[:along], w) for a, w in zip(arrays, widths)], axis=along
    )
    whole = lax.all_gather(both, axis, axis=dim, tiled=True)
    parts = jnp.split(whole, [sum(widths[:k]) for k in range(1, len(widths))], axis=along)
    return tuple((b.reshape(*whole.shape[:along], *a.shape[along:]) for a, b in zip(arrays, parts)))


def sent_to_all(shard, axis):
    size = lax.axis_size(axis)
    return lax.all_to_all(
        jnp.broadcast_to(shard[None], (size, *shard.shape)), axis, 0, 0, tiled=True
    )


def taken_together(shard, axis):
    everything = sent_to_all(shard, axis)
    return jnp.sum(everything, axis=0)


def body(
    train_in,
    train_out,
    query_in,
    query_out,
    query_ids,
    in_basis,
    out_basis,
    level_table,
    in_level,
    out_level,
    lengths,
):
    highest = lax.Precision.HIGHEST
    ex_count = lax.axis_size("ex")
    ex_index = lax.axis_index("ex")
    in_sub = in_basis.shape[0]
    out_sub = out_basis.shape[0]
    width = in_basis.shape[1]
    per_query = in_sub * out_sub
    owned = QUERIES * per_query // ex_count
    block_ids = ex_index * owned + jnp.arange(owned, dtype=jnp.int32)
    query_of = block_ids % QUERIES
    pair_of = block_ids // QUERIES
    out_of = pair_of // in_sub
    in_of = pair_of % in_sub
    out_own = jnp.take(out_basis, out_of, axis=0)
    in_own = jnp.take(in_basis, in_of, axis=0)
    query_code = query_of.astype(jnp.float32)
    piece_in, piece_out, piece_ids = sent_together(
        (query_in, query_out, query_ids.astype(jnp.bfloat16)), "ex", 0, 1
    )
    count = piece_in.shape[0]
    chosen_in = jnp.take(piece_in.reshape(count, in_sub, width), in_of, axis=1)
    chosen_out = jnp.take(piece_out.reshape(count, out_sub, width), out_of, axis=1)
    weights = (piece_ids.astype(jnp.float32)[:, None] == query_code[None, :]).astype(jnp.bfloat16)
    chosen_out = chosen_out * weights[:, :, None]
    grad_own = jnp.einsum("mka,mkb->kab", chosen_out, chosen_in, preferred_element_type=jnp.float32)
    grad_own = grad_own.astype(jnp.bfloat16)
    half = jnp.einsum("kab,kac->kbc", out_own, grad_own, preferred_element_type=jnp.float32).astype(
        jnp.bfloat16
    )
    rotated = jnp.einsum("kbc,kcd->kbd", half, in_own, preferred_element_type=jnp.float32)
    levels = jnp.arange(level_table.shape[0], dtype=jnp.int32)
    out_levels = jnp.take(out_level.reshape(out_sub, width), out_of, axis=0)
    in_levels = jnp.take(in_level.reshape(in_sub, width), in_of, axis=0)
    out_onehot = (out_levels[:, :, None] == levels[None, None, :]).astype(jnp.float32)
    in_onehot = (in_levels[:, :, None] == levels[None, None, :]).astype(jnp.float32)
    partway = jnp.einsum("kbl,lm->kbm", out_onehot, level_table, precision=highest)
    eigen = jnp.einsum("kbm,kdm->kbd", partway, in_onehot, precision=highest)
    damped = (rotated / (eigen + DAMPING)).astype(jnp.bfloat16)
    back = jnp.einsum("kbd,kcd->kbc", damped, in_own, preferred_element_type=jnp.float32).astype(
        jnp.bfloat16
    )
    precond = jnp.einsum("kab,kbc->kac", out_own, back, preferred_element_type=jnp.float32).astype(
        jnp.bfloat16
    )
    tokens = train_in.shape[0]
    in_split = train_in.reshape(tokens, in_sub, width)
    out_split = train_out.reshape(tokens, out_sub, width)
    query_range = jnp.arange(QUERIES, dtype=jnp.int32)
    piece = lax.all_gather(precond, "ex", axis=0, tiled=True)

    def score_one(step, running):
        pair = step // QUERIES
        matrix = lax.dynamic_index_in_dim(piece, step, 0, keepdims=False)
        acts = lax.dynamic_index_in_dim(in_split, pair % in_sub, 1, keepdims=False)
        grads = lax.dynamic_index_in_dim(out_split, pair // in_sub, 1, keepdims=False)
        image = lax.dot_general(
            acts, matrix, (((1,), (1,)), ((), ())), preferred_element_type=jnp.float32
        )
        values = jnp.sum(image * grads.astype(jnp.float32), axis=1)
        selector = (query_range == step % QUERIES).astype(jnp.float32)
        return running + selector[:, None] * values[None, :]

    token_part = lax.fori_loop(
        0, piece.shape[0], score_one, jnp.zeros((QUERIES, tokens), jnp.float32)
    )
    token_scores = taken_together(token_part, ("row", "col"))
    ends = jnp.cumsum(lengths)
    starts = ends - lengths
    positions = ex_index * tokens + jnp.arange(tokens, dtype=jnp.int32)
    member = (
        (positions[None, :] >= starts[:, None]) & (positions[None, :] < ends[:, None])
    ).astype(jnp.float32)
    local_part = lax.dot_general(token_scores, member, (((1,), (1,)), ((), ())), precision=highest)
    example_scores = taken_together(local_part, "ex")
    return (token_scores, example_scores)


def solution(mesh):
    placed = (
        P("ex", "row"),
        P("ex", "col"),
        P("ex", "row"),
        P("ex", "col"),
        P("ex"),
        P("row", None, None),
        P("col", None, None),
        P(),
        P("row"),
        P("col"),
        P(),
    )
    return jax.shard_map(
        body, mesh=mesh, in_specs=placed, out_specs=(P(None, "ex"), P()), check_vma=False
    )
```

profile of v0, /device:TPU:1, one launch (start us, length us, event | category | flops | bytes accessed | tf_op | source)
XLA Modules:
  0.0 416.8 jit_solution(11040072974099691769)
XLA Ops:
  11.9 66.4 %all-gather.4.cloned.1.call-done = bf16[512,6145]{1,0:T(8,128)(2,1)} async-done(((bf16[32,6145]{1,0:T(8,128)(2,1)}), bf16[512,6145]{1,0:T(8,128)(2,1)}) %all-gather.4.cloned.1.call-update) | async-done | bytes 6292496 | tf_op jit(solution)/shard_map/all_gather | solution.py:16
  78.3 4.7 %split.12 = bf16[512,4096]{1,0:T(8,128)(2,1)} slice(bf16[512,6145]{1,0:T(8,128)(2,1)} %all-gather.4.cloned.1.call-done), slice={[0:512], [2048:6144]} | slice | bytes 8388608 | tf_op jit(solution)/shard_map/split | solution.py:17
  83.0 6.5 %copy.58 = bf16[512,4096]{0,1:T(8,128)(2,1)} copy(bf16[512,4096]{1,0:T(8,128)(2,1)} %split.12) | data formatting | bytes 8388608
  96.5 5.5 %fusion.17 = bf16[1024,1024]{1,0:T(8,128)(2,1)S(1)} fusion(bf16[4,1024,1024]{2,1,0:T(8,128)(2,1)} %param.19, s32[]{:T(128)} %bitcast.3, pred[]{:T(512)} %bitcast.2, bf16[512,1,1024]{2,0,1:T(8,128)(2,1)S(1)} %copy.46, bf16[512,2,1024]{0,2,1:T(8,128)(2,1)} %bitcast.75, s32[]{:T(128)} %bitcast.12, pred[]{:T(512)} %bitcast.10, bf16[512]{0:T(512)(128)(2,1)S(1)} %fusion.55), kind=kOutput, calls=%fused_computation.19 | convolution fusion | flops 3224371200 | bytes 6294528 | tf_op jit(solution)/shard_map/kab,kac->kbc/dot_general | solution.py:72
  102.1 3.9 fusion.13
  108.5 8.1 %fusion.22 = bf16[1024,1024]{1,0:T(8,128)(2,1)} fusion(bf16[4,1024,1024]{2,1,0:T(8,128)(2,1)} %param.19, s32[]{:T(128)} %bitcast.3, pred[]{:T(512)} %bitcast.2, bf16[1024,1024]{1,0:T(8,128)(2,1)S(1)} %divide_convert_fusion, bf16[2,1024,1024]{2,1,0:T(8,128)(2,1)} %param.18, s32[]{:T(128)} %bitcast.12, pred[]{:T(512)} %bitcast.10), kind=kOutput, calls=%fused_computation.26 | convolution fusion | flops 4299161600 | bytes 8390656 | tf_op jit(solution)/shard_map/kab,kbc->kac/dot_general | solution.py:87
  116.6 6.7 %copy.49 = bf16[512,4096]{0,1:T(8,128)(2,1)} copy(bf16[512,4096]{1,0:T(8,128)(2,1)} %param.14) | data formatting | bytes 8388608 | tf_op args[1]
  126.1 176.4 %all-gather.6.cloned.1.call-done = bf16[16384,1024]{1,0:T(8,128)(2,1)} async-done(((bf16[1024,1024]{1,0:T(8,128)(2,1)}), bf16[16384,1024]{1,0:T(8,128)(2,1)}) %all-gather.6.cloned.1.call-update) | async-done | bytes 33554448 | tf_op jit(solution)/shard_map/all_gather | solution.py:94
  302.5 84.1 %while.23 = (s32[]{:T(128)}, f32[2,512]{1,0:T(2,128)S(1)}, bf16[512,2,1024]{0,2,1:T(8,128)(2,1)}, bf16[16,1024,1024]{2,1,0:T(8,128)(2,1)}, bf16[512,4,1024]{0,2,...) while((s32[]{:T(128)}, f32[2,512]{1,0:T(2,128)S(1)}, ...), condition=%wide.region_2.3_spmd.clone, body=%wide.region_0.2_spmd.clone.sunk | while | flops 1075317248 | bytes 8401917 | solution.py:108
  304.3 3.3 fusion.80
  309.6 3.3 fusion.80
  314.8 3.3 fusion.80
  320.1 3.3 fusion.80
  330.6 3.3 fusion.80
  335.8 3.3 fusion.80
  341.1 3.3 fusion.80
  346.4 3.3 fusion.80
  367.4 3.3 fusion.80
  372.6 3.3 fusion.80
  377.9 3.3 fusion.80
  383.1 3.3 fusion.80
  387.2 4.2 %all-to-all-start = ((f32[8,2,512]{2,1,0:T(2,128)}), f32[8,2,512]{2,1,0:T(2,128)S(1)}, u32[]{:S(2)}, u32[]{:S(2)}) async-start(f32[8,2,512]{2,1,0:T(2,128)} %broadcast_in_dim.102), calls=%async_computation | async-start | bytes 65536 | tf_op jit(solution)/shard_map/all_to_all | solution.py:23
  391.3 5.1 %all-to-all-done = f32[8,2,512]{2,1,0:T(2,128)S(1)} async-done(((f32[8,2,512]{2,1,0:T(2,128)}), f32[8,2,512]{2,1,0:T(2,128)S(1)}, u32[]{:S(2)}, u32[]{:S(2)}) %all-to-all-start) | async-done | bytes 32800 | tf_op jit(solution)/shard_map/all_to_all | solution.py:23
  396.7 12.6 %all_to_all.10 = f32[16,2,4]{2,1,0:T(2,128)S(1)} all-to-all(f32[16,2,4]{2,1,0:T(2,128)S(1)} %broadcast_in_dim.103), channel_id=1, replica_groups=mesh['row'=4,'col'=2,'ex'=16] {'ex'}, dimensions={0} | all-to-all | bytes 1024 | tf_op jit(solution)/shard_map/all_to_all | solution.py:23
  (107 shorter events, 62.1 us)
Async XLA Ops:
  7.2 4.2 %copy-start = (f32[64,64]{1,0:T(8,128)S(1)}, f32[64,64]{1,0:T(8,128)}, u32[]{:S(2)}) copy-start(f32[64,64]{1,0:T(8,128)} %param.20) | copy-start | bytes 49156
  7.2 71.2 %all-gather.4.cloned.1.call-start = ((), (), s32[]{:S(2)}) async-start(), calls=%async_computation.2 | async-start | bytes 6823936 | tf_op jit(solution)/shard_map/all_gather | solution.py:16
  9.8 292.7 %all-gather.6.cloned.1.call-start = ((), (), s32[]{:S(2)}) async-start(), calls=%async_computation.3 | async-start | bytes 35651584 | tf_op jit(solution)/shard_map/all_gather | solution.py:94
  91.4 1.6 slice-start
  116.6 6.7 %copy-start.2 = (bf16[512,2048]{1,0:T(8,128)(2,1)S(1)}, bf16[512,2048]{1,0:T(8,128)(2,1)}, u32[]{:S(2)}) copy-start(bf16[512,2048]{1,0:T(8,128)(2,1)} %param.13) | copy-start | bytes 6291460
  123.4 2.5 copy-start.4
  386.5 23.4 %copy-start.1 = (f32[64,64]{1,0:T(8,128)S(1)}, f32[64,64]{1,0:T(8,128)}, u32[]{:S(2)}) copy-start(f32[64,64]{1,0:T(8,128)} %param.20) | copy-start | bytes 49156
  387.2 9.3 %all-to-all-start = ((f32[8,2,512]{2,1,0:T(2,128)}), f32[8,2,512]{2,1,0:T(2,128)S(1)}, u32[]{:S(2)}, u32[]{:S(2)}) async-start(f32[8,2,512]{2,1,0:T(2,128)} %broadcast_in_dim.102), calls=%async_computation | async-start | bytes 65536 | tf_op jit(solution)/shard_map/all_to_all | solution.py:23
  396.5 13.5 %copy-start.3 = (f32[2,512]{1,0:T(2,128)}, f32[2,512]{1,0:T(2,128)S(1)}, u32[]{:S(2)}) copy-start(f32[2,512]{1,0:T(2,128)S(1)} %reduce_sum.35) | copy-start | bytes 12292
Sparse Core Ops, SparseCore 0:
  10.4 67.9 all-gather.3
  116.7 185.6 all-gather.5
where the time goes:
time: 418 us; the launch traced here: 417 us
  waiting for transfers between devices  248 us (59%)
  matrix products  73.6 us (18%)
  local copies, waits for them, and re-layouts  56.6 us (14%)
  between operations  14.2 us (3%)
  blocking collectives  12.6 us (3%)
  other arithmetic  6.94 us (2%)
  starting transfers between devices  4.25 us (1%)
    all_gather x1, waiting for transfers between devices, body(): piece = lax.all_gather(precond, 'ex', axis=0, tiled=True)  176 us
    all_gather x1, waiting for transfers between devices, sent_together(): whole = lax.all_gather(both, axis, axis=dim, tiled=True)  66.4 us
    dot_general x16, matrix products, score_one(): lax.dot_general(acts, matrix, (((1,), (1,)), ((), ())), preferred_element...  52.8 us
    dynamic_slice x32, local copies, waits for them, and re-layouts, score_one(): lax.dynamic_index_in_dim(out_split, pair // in_sub, 1, keepdims=False)  29.2 us
    unnamed x14, local copies, waits for them, and re-layouts  18.3 us
    all_to_all x1, blocking collectives, sent_to_all(): lax.all_to_all(jnp.broadcast_to(shard[None], (size, *shard.shape)), axis,...  12.6 us
  transfers between devices with their start and end apart: 3, of which 3 were waited for; matrix products, arithmetic and copies ran while one was open for 3% of the time, Pallas kernels for 0%

commit v1 on v0

--- a/solution.py
+++ b/solution.py
@@ -91,7 +91,9 @@
     in_split = train_in.reshape(tokens, in_sub, width)
     out_split = train_out.reshape(tokens, out_sub, width)
     query_range = jnp.arange(QUERIES, dtype=jnp.int32)
-    piece = lax.all_gather(precond, "ex", axis=0, tiled=True)
+    piece = jnp.concatenate(
+        lax.all_to_all(jnp.stack([precond] * lax.axis_size("ex")), "ex", 0, 0), axis=0
+    )
 
     def score_one(step, running):
         pair = step // QUERIES

time: 418 us -> 806 us (1.93)
  waiting for transfers between devices: 248 us -> 611 us
  local copies, waits for them, and re-layouts: 56.6 us -> 67.6 us
    all_to_all x0 -> x1, waiting for transfers between devices: none -> 539 us  [body(): lax.all_to_all(jnp.stack([precond] * lax.axis_size('ex')), 'ex', 0, 0)]
    all_gather x1 -> x0, waiting for transfers between devices: 176 us -> none  [body(): piece = lax.all_gather(precond, 'ex', axis=0, tiled=True)]
    another operation x0 -> x1, local copies, waits for them, and re-layouts: none -> 11.1 us  [body(): jnp.stack([precond] * lax.axis_size('ex'))]
  transfers between devices with their start and end apart: 3 -> 3, of which waited for: 3 -> 3; matrix products, arithmetic and copies ran while one was open for 3% -> 1% of each run, Pallas kernels for 0% -> 0%
where the time goes in v1:
time: 806 us; the launch traced here: 804 us
  waiting for transfers between devices  611 us (76%)
  matrix products  74.3 us (9%)
  local copies, waits for them, and re-layouts  67.6 us (8%)
  blocking collectives  19.1 us (2%)
  between operations  14.2 us (2%)
  starting transfers between devices  10.3 us (1%)
    all_to_all x1, waiting for transfers between devices, body(): lax.all_to_all(jnp.stack([precond] * lax.axis_size('ex')), 'ex', 0, 0)  539 us
    all_gather x1, waiting for transfers between devices, sent_together(): whole = lax.all_gather(both, axis, axis=dim, tiled=True)  66.5 us
    dot_general x16, matrix products, score_one(): lax.dot_general(acts, matrix, (((1,), (1,)), ((), ())), preferred_element...  52.8 us
    dynamic_slice x32, local copies, waits for them, and re-layouts, score_one(): lax.dynamic_index_in_dim(out_split, pair // in_sub, 1, keepdims=False)  29.2 us
    all_to_all x1, blocking collectives, sent_to_all(): lax.all_to_all(jnp.broadcast_to(shard[None], (size, *shard.shape)), axis,...  19.1 us
    unnamed x14, local copies, waits for them, and re-layouts  18.3 us
  transfers between devices with their start and end apart: 3, of which 3 were waited for; matrix products, arithmetic and copies ran while one was open for 1% of the time, Pallas kernels for 0%

profile of v1, /device:TPU:1, one launch (start us, length us, event | category | flops | bytes accessed | tf_op | source)
XLA Modules:
  0.0 804.0 jit_solution(17859401809099584376)
XLA Ops:
  11.9 66.5 %all-gather.2.cloned.1.call-done = bf16[512,6145]{1,0:T(8,128)(2,1)} async-done(((bf16[32,6145]{1,0:T(8,128)(2,1)}), bf16[512,6145]{1,0:T(8,128)(2,1)}) %all-gather.2.cloned.1.call-update) | async-done | bytes 6292496 | tf_op jit(solution)/shard_map/all_gather | solution.py:16
  78.3 4.7 split.12
  83.1 6.5 copy.58
  96.6 5.5 fusion.17
  102.1 3.9 fusion.13
  106.0 3.8 divide_convert_fusion
  109.9 7.4 fusion.22
  117.3 11.1 %stack.2 = bf16[16,1,1024,1024]{3,2,1,0:T(8,128)(2,1)} broadcast(bf16[1024,1024]{1,0:T(8,128)(2,1)S(1)} %fusion.22), dimensions={2,3} | broadcast | bytes 35651584 | tf_op jit(solution)/shard_map/stack | solution.py:95
  128.4 6.1 all-to-all-start
  134.5 6.7 copy.49
  143.9 539.4 %all-to-all-done = bf16[16,1,1024,1024]{3,2,1,0:T(8,128)(2,1)} async-done(((bf16[16,1,1024,1024]{3,2,1,0:T(8,128)(2,1)}), bf16[16,1,1024,1024]{3,2,1,0:T(8,128)(2,1)}, u32[]{:S(2)}, u32[]{:S(2)}) %all-to-all-start) | async-done | bytes 33554464 | tf_op jit(solution)/shard_map/all_to_all | solution.py:95
  683.3 84.1 %while.23 = (s32[]{:T(128)}, f32[2,512]{1,0:T(2,128)S(1)}, bf16[512,2,1024]{0,2,1:T(8,128)(2,1)}, bf16[16,1024,1024]{2,1,0:T(8,128)(2,1)}, bf16[512,4,1024]{0,2,...) while((s32[]{:T(128)}, f32[2,512]{1,0:T(2,128)S(1)}, ...), condition=%wide.region_2.3_spmd.clone, body=%wide.region_0.2_spmd.clone.sunk | while | flops 1075317248 | bytes 8401917 | solution.py:110
  685.1 3.3 fusion.80
  690.4 3.3 fusion.80
  695.6 3.3 fusion.80
  700.9 3.3 fusion.80
  716.7 3.3 fusion.80
  721.9 3.3 fusion.80
  727.2 3.3 fusion.80
  732.4 3.3 fusion.80
  748.2 3.3 fusion.80
  768.0 4.2 all-to-all-start.1
  772.2 5.1 all-to-all-done.1
  777.5 19.1 %all_to_all.15 = f32[16,2,4]{2,1,0:T(2,128)S(1)} all-to-all(f32[16,2,4]{2,1,0:T(2,128)S(1)} %broadcast_in_dim.103), channel_id=1, replica_groups=mesh['row'=4,'col'=2,'ex'=16] {'ex'}, dimensions={0} | all-to-all | bytes 1024 | tf_op jit(solution)/shard_map/all_to_all | solution.py:23
  (107 shorter events, 69.5 us)
Async XLA Ops:
  7.2 4.1 copy-start
  7.2 71.2 %all-gather.2.cloned.1.call-start = ((), (), s32[]{:S(2)}) async-start(), calls=%async_computation.3 | async-start | bytes 6823936 | tf_op jit(solution)/shard_map/all_gather | solution.py:16
  91.4 1.6 slice-start
  128.4 554.9 %all-to-all-start = ((bf16[16,1,1024,1024]{3,2,1,0:T(8,128)(2,1)}), bf16[16,1,1024,1024]{3,2,1,0:T(8,128)(2,1)}, u32[]{:S(2)}, u32[]{:S(2)}) async-start(bf16[16,1,1024,1024]{3,2,1,0:T(8,128)(2,1)} %stack.2), calls=%async_computation | async-start | bytes 67108864 | tf_op jit(solution)/shard_map/all_to_all | solution.py:95
  134.5 6.7 copy-start.2
  141.2 2.5 copy-start.4
  767.4 29.8 %copy-start.1 = (f32[64,64]{1,0:T(8,128)S(1)}, f32[64,64]{1,0:T(8,128)}, u32[]{:S(2)}) copy-start(f32[64,64]{1,0:T(8,128)} %param.20) | copy-start | bytes 49156
  768.0 9.3 %all-to-all-start.1 = ((f32[8,2,512]{2,1,0:T(2,128)}), f32[8,2,512]{2,1,0:T(2,128)S(1)}, u32[]{:S(2)}, u32[]{:S(2)}) async-start(f32[8,2,512]{2,1,0:T(2,128)} %broadcast_in_dim.102), calls=%async_computation.1 | async-start | bytes 65536 | tf_op jit(solution)/shard_map/all_to_all | solution.py:23
  777.3 19.9 %copy-start.3 = (f32[2,512]{1,0:T(2,128)}, f32[2,512]{1,0:T(2,128)S(1)}, u32[]{:S(2)}) copy-start(f32[2,512]{1,0:T(2,128)S(1)} %reduce_sum.35) | copy-start | bytes 12292
Sparse Core Ops, SparseCore 0:
  10.4 67.9 all-gather.1
